TPU v7x, 32 devices: a whole 2x2x4 slice. The times are simulated.
32 devices in a mesh: tm: 8 (over z, y), row: 2 (over core), col: 2 (over x).
Axes of the slice: x: 2, y: 2, z: 4, core: 2. Of those that a mesh axis runs over, the one named last changes fastest.
Arguments:
- precision_diag: float32 [16, 512, 512], P('tm', 'row', 'col'), may hold values from -4 to 16
- precision_link: float32 [16, 512, 512], P('tm', 'row', 'col'), may hold values from -8 to 2
Outputs:
- pivots: float32 [16, 512, 512], P('tm', 'row', 'col')
- couplings: float32 [16, 512, 512], P('tm', 'row', 'col')
- log_variance: float32 [16, 512], P('tm', ('row', 'col'))
All inputs are finite; a program needn't handle non-finite values.
Results may differ from a plain program's by a relative error of at most 0.0003.
Values sent between devices are 32-bit elements; how exact they have to be, the bound alone decides.
A program may use at most 128 MiB of HBM per device.

v0:
```python
import jax
import jax.numpy as jnp
from jax import lax
from jax.sharding import PartitionSpec as P

LEVELS = 4


def shifted(array, axis, by):
    devices = lax.axis_size(axis)
    pairs = [(i, i + by) for i in range(devices) if 0 <= i + by < devices]
    return lax.ppermute(array, axis, pairs)


def product_tn(left_part, right_part):
    return jnp.einsum("ki,kl->il", left_part, right_part, precision=lax.Precision.HIGHEST)


def factor_solve(pivot, right_side):
    lower_factor = jnp.linalg.cholesky(pivot)
    return jax.scipy.linalg.solve_triangular(lower_factor, right_side, lower=True)


def unit_columns(node_count, diag_id):
    quarter = node_count // 4
    row_positions = jnp.arange(node_count)[:, None]
    col_positions = diag_id * quarter + jnp.arange(quarter)[None, :]
    return (row_positions == col_positions).astype(jnp.float32)


def log_variance(inverse_cols):
    return jnp.log(jnp.sum(inverse_cols * inverse_cols, axis=0))


def column_half(panel, index_id):
    half_width = panel.shape[1] // 2
    return lax.dynamic_slice_in_dim(panel, index_id * half_width, half_width, 1)


def whole_blocks(stacked):
    widened = lax.all_gather(stacked, "col", axis=2, tiled=True)
    return lax.all_gather(widened, "row", axis=1, tiled=True)


def send_later(gram_up, link_new, stride):
    return shifted((gram_up, link_new), "tm", stride)


def guarded(active, compute, zero_fill, operands):
    if active is None:
        return compute(operands)
    return lax.cond(active, compute, zero_fill, operands)


def solve_divided(operands, place):
    row_id, col_id, diag_id = place
    pivot, below_cols, above_rows = operands
    node_count = pivot.shape[0]
    half_width = below_cols.shape[1]
    right_side = jnp.concatenate(
        [below_cols, above_rows.T, unit_columns(node_count, diag_id)], axis=1
    )
    solved = factor_solve(pivot, right_side)
    lower_own = solved[:, :half_width]
    upper_own = solved[:, half_width : 2 * half_width]
    log_part = log_variance(solved[:, 2 * half_width :])
    return (log_part, lower_own, upper_own, -product_tn(upper_own, lower_own))


def gram_divided(panels, place):
    row_id, col_id, diag_id = place
    lower_whole, upper_whole = panels
    return (
        product_tn(column_half(lower_whole, row_id), column_half(lower_whole, col_id)),
        product_tn(column_half(upper_whole, row_id), column_half(upper_whole, col_id)),
    )


def eliminate(pivot_tile, below_tile, above_tile, active, place):
    half_width = pivot_tile.shape[0]
    node_count = 2 * half_width
    log_zero = jnp.zeros((node_count // 4,), jnp.float32)
    tile_zero = jnp.zeros((half_width, half_width), jnp.float32)
    pivot = whole_blocks(pivot_tile[None])[0]
    below_cols = lax.all_gather(below_tile, "row", axis=0, tiled=True)
    above_rows = lax.all_gather(above_tile, "col", axis=1, tiled=True)
    panel_zero = jnp.zeros((node_count, half_width), jnp.float32)
    log_part, lower_own, upper_own, link_new = guarded(
        active,
        lambda operands: solve_divided(operands, place),
        lambda operands: (log_zero, panel_zero, panel_zero, tile_zero),
        (pivot, below_cols, above_rows),
    )
    lower_whole = lax.all_gather(lower_own, "col", axis=1, tiled=True)
    upper_whole = lax.all_gather(upper_own, "row", axis=1, tiled=True)
    gram_down, gram_up = guarded(
        active,
        lambda operands: gram_divided(operands, place),
        lambda operands: (tile_zero, tile_zero),
        (lower_whole, upper_whole),
    )
    return (log_part, gram_down, gram_up, link_new)


def final_log(pivot, place):
    row_id, col_id, diag_id = place
    inverse_cols = factor_solve(pivot, unit_columns(pivot.shape[0], diag_id))
    return log_variance(inverse_cols)


def shards(precision_diag, precision_link):
    row_id = lax.axis_index("row")
    col_id = lax.axis_index("col")
    time_id = lax.axis_index("tm")
    place = (row_id, col_id, row_id * 2 + col_id)
    device_count = lax.axis_size("tm")
    pivot_low = precision_diag[0]
    pivot_high = precision_diag[1]
    link_low = precision_link[0]
    link_high = jnp.where(
        time_id == device_count - 1, jnp.zeros_like(precision_link[1]), precision_link[1]
    )
    log_high, gram_down, gram_up, link_low = eliminate(pivot_high, link_low, link_high, None, place)
    ahead_gram, from_below = send_later(gram_up, link_low, 1)
    pivot_low = pivot_low - gram_down - ahead_gram
    log_low = jnp.zeros_like(log_high)
    for level_num in range(1, LEVELS):
        stride = 2 ** (level_num - 1)
        position = time_id % (2 * stride)
        active = position == stride
        keeper = position == 0
        below_link = from_below
        log_now, gram_down, gram_up, link_new = eliminate(
            pivot_low, below_link, link_low, active, place
        )
        back_gram, back_link = shifted((gram_down, link_new), "tm", -stride)
        ahead_gram, from_below = send_later(gram_up, link_new, stride)
        log_low = jnp.where(active, log_now, log_low)
        pivot_low = pivot_low - back_gram - ahead_gram
        link_low = jnp.where(keeper, back_link, link_low)
    remaining = time_id % 2 ** (LEVELS - 1) == 0
    whole_pivot = whole_blocks(pivot_low[None])[0]
    log_final = lax.cond(
        remaining,
        lambda pivot: final_log(pivot, place),
        lambda pivot: jnp.zeros_like(log_low),
        whole_pivot,
    )
    log_low = jnp.where(remaining, log_final, log_low)
    pivots = jnp.stack([pivot_low, pivot_high])
    couplings = jnp.stack([link_low, link_high])
    logs = jnp.stack([log_low, log_high])
    return (pivots, couplings, logs)


def solution(mesh):
    in_specs = (P("tm", "row", "col"), P("tm", "row", "col"))
    out_specs = (P("tm", "row", "col"), P("tm", "row", "col"), P("tm", ("row", "col")))
    return jax.shard_map(shards, mesh=mesh, in_specs=in_specs, out_specs=out_specs, check_vma=False)
```

profile of v0, /device:TPU:0, one launch (start us, length us, event | category | flops | bytes accessed | tf_op | source)
XLA Modules:
  0.0 1136.3 jit_solution(9765226666093898980)
XLA Ops:
  9.2 10.0 all_gather.78
  36.1 11.7 %cholesky.838 = f32[128,128]{1,0:T(8,128)S(1)} custom-call(f32[128,128]{1,0:T(8,128)S(1)} %cholesky.958), custom_call_target="Cholesky" | custom-call | tf_op jit(solution)/shard_map/jit(cholesky)/cholesky | solution.py:20
  60.3 11.7 %cholesky.857 = f32[128,128]{1,0:T(8,128)S(1)} custom-call(f32[128,128]{1,0:T(8,128)S(1)} %cholesky.962), custom_call_target="Cholesky" | custom-call | tf_op jit(solution)/shard_map/jit(cholesky)/cholesky | solution.py:20
  72.1 10.1 custom-call.58
  83.8 11.7 %cholesky.878 = f32[128,128]{1,0:T(8,128)S(1)} custom-call(f32[128,128]{1,0:T(8,128)S(1)} %cholesky.967), custom_call_target="Cholesky" | custom-call | tf_op jit(solution)/shard_map/jit(cholesky)/cholesky | solution.py:20
  107.5 11.7 %cholesky.895 = f32[128,128]{1,0:T(8,128)S(1)} custom-call(f32[128,128]{1,0:T(8,128)S(1)} %convolution_subtract_fusion.30), custom_call_target="Cholesky" | custom-call | tf_op jit(solution)/shard_map/jit(cholesky)/cholesky | solution.py:20
  124.5 11.6 %while.13 = (s32[]{:T(128)}, f32[512,512]{1,0:T(8,128)}, s32[4,2]{0,1:T(2,128)S(1)}, f32[4,128,128]{2,1,0:T(8,128)S(1)}, s32[]{:T(128)}) while((s32[]{:T(128)}, f32[512,512]{1,0:T(8,128)}, s32[4,2]{0,1:T(2,128)S(1)}, f32[4,128,128]{2,1,0:T(8,128)S(1)}, s32[]{:T(128)}) %tuple.211), condition=%wide.while_cond.clone.2, body=%wide.while_body.clone.2.sunk | while | flops 2 | bytes 131189 | solution.py:21
  136.1 39.3 %custom-call.60 = f32[4,128,128]{1,2,0:T(8,128)S(1)} custom-call(f32[4,128,128]{2,1,0:T(8,128)S(1)} %get-tuple-element.163), custom_call_target="InvertDiagBlocksLowerTriangular" | custom-call | tf_op jit(solution)/shard_map/jit(_solve_triangular)/triangular_solve | solution.py:21
  185.9 9.9 all-gather.28.cloned.1.call-done
  201.9 18.5 %all-gather.26.cloned.1.call-done = f32[512,512]{1,0:T(8,128)} async-done(((f32[512,256]{1,0:T(8,128)}), f32[512,512]{1,0:T(8,128)}) %all-gather.26.cloned.1.call-update) | async-done | bytes 1048592 | tf_op jit(solution)/shard_map/all_gather | solution.py:94
  251.0 184.8 %all-gather.30.cloned.1.call-done = f32[512,512]{1,0:T(8,128)} async-done(((f32[512,256]{1,0:T(8,128)}), f32[512,512]{1,0:T(8,128)}) %all-gather.30.cloned.1.call-update) | async-done | bytes 1048592 | tf_op jit(solution)/shard_map/all_gather | solution.py:94
  435.8 11.0 all-gather.32.cloned.1.call-done
  455.6 10.3 collective-permute-done.3
  499.0 192.1 %all-gather.34.cloned.1.call-done = f32[512,512]{1,0:T(8,128)} async-done(((f32[512,256]{1,0:T(8,128)}), f32[512,512]{1,0:T(8,128)}) %all-gather.34.cloned.1.call-update) | async-done | bytes 1048592 | tf_op jit(solution)/shard_map/all_gather | solution.py:94
  691.1 11.2 all-gather.36.cloned.1.call-done
  752.4 184.5 %all-gather.38.cloned.1.call-done = f32[512,512]{1,0:T(8,128)} async-done(((f32[512,256]{1,0:T(8,128)}), f32[512,512]{1,0:T(8,128)}) %all-gather.38.cloned.1.call-update) | async-done | bytes 1048592 | tf_op jit(solution)/shard_map/all_gather | solution.py:94
  936.9 11.0 all-gather.40.cloned.1.call-done
  992.0 136.6 %conditional.13 = (f32[128]{0:T(128)S(1)}) conditional(s32[]{:T(128)} %convert_element_type.34, () %tuple.76, (f32[1,512,512]{1,2,0:T(8,128)}, s32[]{:T(128)}) %tuple.257), branch_computations={%region_23.26_spmd, %region_24.28_spmd} | conditional | flops 656916992 | bytes 27548512 | solution.py:143
  995.2 11.7 %cholesky.766 = f32[128,128]{1,0:T(8,128)S(1)} custom-call(f32[128,128]{1,0:T(8,128)S(1)} %cholesky.919), custom_call_target="Cholesky" | custom-call | tf_op jit(solution)/shard_map/cond/branch_1_fun/jit(cholesky)/cholesky | solution.py:20
  1017.6 11.7 %cholesky.785 = f32[128,128]{1,0:T(8,128)S(1)} custom-call(f32[128,128]{1,0:T(8,128)S(1)} %cholesky.923), custom_call_target="Cholesky" | custom-call | tf_op jit(solution)/shard_map/cond/branch_1_fun/jit(cholesky)/cholesky | solution.py:20
  1031.3 10.0 custom-call.55
  1042.0 11.7 %cholesky.806 = f32[128,128]{1,0:T(8,128)S(1)} custom-call(f32[128,128]{1,0:T(8,128)S(1)} %cholesky.928), custom_call_target="Cholesky" | custom-call | tf_op jit(solution)/shard_map/cond/branch_1_fun/jit(cholesky)/cholesky | solution.py:20
  1065.4 11.7 %cholesky.823 = f32[128,128]{1,0:T(8,128)S(1)} custom-call(f32[128,128]{1,0:T(8,128)S(1)} %convolution_subtract_fusion.11), custom_call_target="Cholesky" | custom-call | tf_op jit(solution)/shard_map/cond/branch_1_fun/jit(cholesky)/cholesky | solution.py:20
  1087.0 39.3 %custom-call.26 = f32[4,128,128]{1,2,0:T(8,128)S(1)} custom-call(f32[4,128,128]{2,1,0:T(8,128)S(1)} %get-tuple-element.141), custom_call_target="InvertDiagBlocksLowerTriangular" | custom-call | tf_op jit(solution)/shard_map/cond/branch_1_fun/jit(_solve_triangular)/triangular_solve | solution.py:21
  (277 shorter events, 292.2 us)
Async XLA Ops:
  7.2 23.8 %all-gather.24.cloned.1.call-start = ((), (), s32[]{:S(2)}) async-start(), calls=%async_computation | async-start | bytes 1572864 | tf_op jit(solution)/shard_map/all_gather | solution.py:42
  19.2 176.6 %all-gather.28.cloned.1.call-start = ((), (), s32[]{:S(2)}) async-start(), calls=%async_computation.2 | async-start | bytes 1572864 | tf_op jit(solution)/shard_map/all_gather | solution.py:95
  185.1 35.3 %all-gather.26.cloned.1.call-start = ((), (), s32[]{:S(2)}) async-start(), calls=%async_computation.1 | async-start | bytes 1572864 | tf_op jit(solution)/shard_map/all_gather | solution.py:94
  185.8 59.5 %all-gather.42.cloned.1.call-start = ((), (), s32[]{:S(2)}) async-start(), calls=%async_computation.9 | async-start | bytes 1572864 | tf_op jit(solution)/shard_map/all_gather | solution.py:42
  198.1 22.3 %collective-permute-start = (f32[256,256]{0,1:T(8,128)S(1)}, f32[256,256]{0,1:T(8,128)S(1)}, u32[]{:S(2)}, u32[]{:S(2)}) collective-permute-start(f32[256,256]{0,1:T(8,128)S(1)} %fusion.162), channel_id=1, source_target_pairs={{0,4},{4,8},{8,12},{12,16},{16,20},{20,24},{24,28},{1,5},{5,9},{9,... | collective-permute-start | bytes 786440 | tf_op jit(solution)/shard_map/ppermute | solution.py:12
  231.3 204.5 %all-gather.30.cloned.1.call-start = ((), (), s32[]{:S(2)}) async-start(), calls=%async_computation.3 | async-start | bytes 1572864 | tf_op jit(solution)/shard_map/all_gather | solution.py:94
  232.4 10.7 collective-permute-start.1
  250.4 196.5 %all-gather.32.cloned.1.call-start = ((), (), s32[]{:S(2)}) async-start(), calls=%async_computation.4 | async-start | bytes 1572864 | tf_op jit(solution)/shard_map/all_gather | solution.py:95
  250.9 242.4 %all-gather.44.cloned.1.call-start = ((), (), s32[]{:S(2)}) async-start(), calls=%async_computation.10 | async-start | bytes 1572864 | tf_op jit(solution)/shard_map/all_gather | solution.py:42
  447.2 18.7 %collective-permute-start.3 = (f32[256,256]{0,1:T(8,128)S(1)}, f32[256,256]{0,1:T(8,128)S(1)}, u32[]{:S(2)}, u32[]{:S(2)}) collective-permute-start(f32[256,256]{0,1:T(8,128)S(1)} %copy.17), channel_id=1, source_target_pairs={{0,4},{4,8},{8,12},{12,16},{16,20},{20,24},{24,28},{1,5},{5,9},{9,... | collective-permute-start | bytes 786440 | tf_op jit(solution)/shard_map/ppermute | solution.py:12
  454.3 11.6 %collective-permute-start.2 = (f32[256,256]{0,1:T(8,128)S(1)}, f32[256,256]{0,1:T(8,128)S(1)}, u32[]{:S(2)}, u32[]{:S(2)}) collective-permute-start(f32[256,256]{0,1:T(8,128)S(1)} %copy.16), channel_id=1, source_target_pairs={{4,0},{8,4},{12,8},{16,12},{20,16},{24,20},{28,24},{5,1},{9,5},{13... | collective-permute-start | bytes 786440 | tf_op jit(solution)/shard_map/ppermute | solution.py:12
  474.5 216.6 %all-gather.34.cloned.1.call-start = ((), (), s32[]{:S(2)}) async-start(), calls=%async_computation.5 | async-start | bytes 1572864 | tf_op jit(solution)/shard_map/all_gather | solution.py:94
  476.0 15.1 %collective-permute-start.5 = (f32[256,256]{0,1:T(8,128)S(1)}, f32[256,256]{0,1:T(8,128)S(1)}, u32[]{:S(2)}, u32[]{:S(2)}) collective-permute-start(f32[256,256]{0,1:T(8,128)S(1)} %copy.18), channel_id=1, source_target_pairs={{0,4},{4,8},{8,12},{12,16},{16,20},{20,24},{24,28},{1,5},{5,9},{9,... | collective-permute-start | bytes 786440 | tf_op jit(solution)/shard_map/ppermute | solution.py:12
  498.3 204.0 %all-gather.36.cloned.1.call-start = ((), (), s32[]{:S(2)}) async-start(), calls=%async_computation.6 | async-start | bytes 1572864 | tf_op jit(solution)/shard_map/all_gather | solution.py:95
  499.0 247.7 %all-gather.46.cloned.1.call-start = ((), (), s32[]{:S(2)}) async-start(), calls=%async_computation.11 | async-start | bytes 1572864 | tf_op jit(solution)/shard_map/all_gather | solution.py:42
  702.6 13.1 %collective-permute-start.7 = (f32[256,256]{0,1:T(8,128)S(1)}, f32[256,256]{0,1:T(8,128)S(1)}, u32[]{:S(2)}, u32[]{:S(2)}) collective-permute-start(f32[256,256]{0,1:T(8,128)S(1)} %copy.20), channel_id=1, source_target_pairs={{0,8},{4,12},{8,16},{12,20},{16,24},{20,28},{1,9},{5,13},{9,17},{1... | collective-permute-start | bytes 786440 | tf_op jit(solution)/shard_map/ppermute | solution.py:12
  709.7 10.1 collective-permute-start.6
  728.8 208.1 %all-gather.38.cloned.1.call-start = ((), (), s32[]{:S(2)}) async-start(), calls=%async_computation.7 | async-start | bytes 1572864 | tf_op jit(solution)/shard_map/all_gather | solution.py:94
  730.3 14.1 %collective-permute-start.9 = (f32[256,256]{0,1:T(8,128)S(1)}, f32[256,256]{0,1:T(8,128)S(1)}, u32[]{:S(2)}, u32[]{:S(2)}) collective-permute-start(f32[256,256]{0,1:T(8,128)S(1)} %copy.21), channel_id=1, source_target_pairs={{0,8},{4,12},{8,16},{12,20},{16,24},{20,28},{1,9},{5,13},{9,17},{1... | collective-permute-start | bytes 786440 | tf_op jit(solution)/shard_map/ppermute | solution.py:12
  751.7 196.2 %all-gather.40.cloned.1.call-start = ((), (), s32[]{:S(2)}) async-start(), calls=%async_computation.8 | async-start | bytes 1572864 | tf_op jit(solution)/shard_map/all_gather | solution.py:95
  752.3 239.7 %all-gather.48.cloned.1.call-start = ((), (), s32[]{:S(2)}) async-start(), calls=%async_computation.12 | async-start | bytes 1572864 | tf_op jit(solution)/shard_map/all_gather | solution.py:42
  948.3 14.1 %collective-permute-start.11 = (f32[256,256]{0,1:T(8,128)S(1)}, f32[256,256]{0,1:T(8,128)S(1)}, u32[]{:S(2)}, u32[]{:S(2)}) collective-permute-start(f32[256,256]{0,1:T(8,128)S(1)} %copy.23), channel_id=1, source_target_pairs={{0,16},{4,20},{8,24},{12,28},{1,17},{5,21},{9,25},{13,29},{2,18},{... | collective-permute-start | bytes 786440 | tf_op jit(solution)/shard_map/ppermute | solution.py:12
  956.3 14.3 %collective-permute-start.10 = (f32[256,256]{0,1:T(8,128)S(1)}, f32[256,256]{0,1:T(8,128)S(1)}, u32[]{:S(2)}, u32[]{:S(2)}) collective-permute-start(f32[256,256]{0,1:T(8,128)S(1)} %copy.22), channel_id=1, source_target_pairs={{16,0},{20,4},{24,8},{28,12},{17,1},{21,5},{25,9},{29,13},{18,2},{... | collective-permute-start | bytes 786440 | tf_op jit(solution)/shard_map/ppermute | solution.py:12
  979.8 10.3 collective-permute-start.12
  (31 other events, 820.6 us)
Sparse Core Ops, SparseCore 0:
  19.4 10.5 all-gather.23
  185.2 10.5 all-gather.27
  197.9 22.4 all-gather.25
  231.4 9.0 all-gather.41
  250.5 185.3 all-gather.29
  437.8 9.0 all-gather.31
  474.6 10.2 all-gather.43
  498.4 192.6 all-gather.33
  693.2 9.0 all-gather.35
  728.9 8.0 all-gather.45
  751.9 184.9 all-gather.37
  938.9 9.0 all-gather.39
  979.9 6.2 all-gather.47
where the time goes:
time: 1150 us; the launch traced here: 1140 us
  waiting for transfers between devices  672 us (58%)
  other arithmetic  242 us (21%)
  blocking collectives  83.7 us (7%)
  starting transfers between devices  47.2 us (4%)
  local copies, waits for them, and re-layouts  37.3 us (3%)
  matrix products  23.3 us (2%)
  between operations  18.1 us (2%)
  loops' own time  13.3 us (1%)
    all_gather x4, waiting for transfers between devices, eliminate(): lower_whole = lax.all_gather(lower_own, 'col', axis=1, tiled=True)  580 us
    another operation x28, other arithmetic, factor_solve(): lower_factor = jnp.linalg.cholesky(pivot)  157 us
    another operation x8, other arithmetic, factor_solve(): jax.scipy.linalg.solve_triangular(lower_factor, right_side, lower=True)  80.2 us
    ppermute x13, starting transfers between devices, shifted(): return lax.ppermute(array, axis, pairs)  46.7 us
    ppermute x13, waiting for transfers between devices, shifted(): return lax.ppermute(array, axis, pairs)  46.3 us
    all_gather x5, blocking collectives, whole_blocks(): widened = lax.all_gather(stacked, 'col', axis=2, tiled=True)  44.3 us
    all_gather x4, waiting for transfers between devices, eliminate(): upper_whole = lax.all_gather(upper_own, 'row', axis=1, tiled=True)  43.2 us
    all_gather x4, blocking collectives, eliminate(): above_rows = lax.all_gather(above_tile, 'col', axis=1, tiled=True)  30.4 us
  transfers between devices with their start and end apart: 26, of which 16 were waited for; matrix products, arithmetic and copies ran while one was open for 1% of the time, Pallas kernels for 0%

commit v1 on v0

v1 whole, which is shorter than its diff:
```python
import jax
import jax.numpy as jnp
from jax import lax
from jax.experimental import pallas as pl
from jax.experimental.pallas import tpu as pltpu
from jax.sharding import PartitionSpec as P

LEVELS = 4


def shifted(array, axis, by):
    devices = lax.axis_size(axis)
    pairs = [(i, i + by) for i in range(devices) if 0 <= i + by < devices]
    return lax.ppermute(array, axis, pairs)


LANES = 128
ROWS = 8


def hdot(left, right, dims=((1,), (0,))):
    return lax.dot_general(
        left, right, (dims, ((), ())), precision=lax.Precision.HIGHEST, preferred_element_type=jnp.float32
    )


def invert_lanes(block):
    sub = lax.broadcasted_iota(jnp.int32, (ROWS, LANES), 0)
    lane = lax.broadcasted_iota(jnp.int32, (ROWS, LANES), 1)
    strips = [block[ROWS * q : ROWS * (q + 1), :] for q in range(LANES // ROWS)]
    for p in range(len(strips)):
        base = ROWS * p
        spread = lambda strip: [
            jnp.broadcast_to(strip[:, base + j : base + j + 1], (ROWS, LANES)) for j in range(ROWS)
        ]
        inside = (lane >= base) & (lane < base + ROWS)
        panel = strips[p]
        cols = spread(panel)
        panel = jnp.where(inside, jnp.where(lane - base == sub, 1.0, 0.0), panel)
        for i in range(ROWS):
            here = sub == i
            scale = 1.0 / jnp.broadcast_to(cols[i][i : i + 1, :], (ROWS, LANES))
            factor = jnp.where(here, scale, -cols[i] * scale)
            panel = jnp.where(here, 0.0, panel) + factor * panel[i : i + 1, :]
            for j in range(i + 1, ROWS):
                cols[j] = jnp.where(here, 0.0, cols[j]) + factor * cols[j][i : i + 1, :]
        order = [q for q in range(p + 1, len(strips))] + [q for q in range(p)]
        for q in order:
            terms = [c * panel[j : j + 1, :] for j, c in enumerate(spread(strips[q]))]
            while len(terms) > 1:
                terms = [terms[m] + terms[m + 1] for m in range(0, len(terms), 2)]
            strips[q] = jnp.where(inside, 0.0, strips[q]) - terms[0]
        strips[p] = panel
    return jnp.concatenate(strips, axis=0)


def invert_ref(work):
    node_count = work.shape[0]

    def step(k, carry):
        here = pl.ds(pl.multiple_of(k * LANES, LANES), LANES)
        inverse = invert_lanes(work[here, here])
        solved = hdot(inverse, work[here, :])
        column = work[:, here]
        work[:, here] = jnp.zeros((node_count, LANES), jnp.float32)
        row_block = lax.broadcasted_iota(jnp.int32, (node_count, LANES), 0) // LANES
        column = jnp.where(row_block == k, 0.0, column)
        col_block = lax.broadcasted_iota(jnp.int32, (LANES, node_count), 1) // LANES
        wide = jnp.concatenate([inverse] * (node_count // LANES), axis=1)
        solved = jnp.where(col_block == k, wide, solved)
        work[...] = work[...] - hdot(column, solved)
        work[here, :] = solved
        return carry

    lax.fori_loop(0, node_count // LANES, step, 0)


def inverse_kernel(pivot_ref, inverse_ref):
    inverse_ref[...] = pivot_ref[...]
    invert_ref(inverse_ref)


def inverse_of(pivot):
    return pl.pallas_call(
        inverse_kernel,
        out_shape=jax.ShapeDtypeStruct(pivot.shape, jnp.float32),
        in_specs=[pl.BlockSpec(memory_space=pltpu.VMEM)],
        out_specs=pl.BlockSpec(memory_space=pltpu.VMEM),
    )(pivot)


def log_of(inverse, place):
    quarter = inverse.shape[0] // 4
    return lax.dynamic_slice_in_dim(jnp.log(jnp.diagonal(inverse)), place[2] * quarter, quarter, 0)


def whole_blocks(stacked):
    widened = lax.all_gather(stacked, "col", axis=2, tiled=True)
    return lax.all_gather(widened, "row", axis=1, tiled=True)


def send_later(gram_up, link_new, stride):
    return shifted((gram_up, link_new), "tm", stride)


def guarded(active, compute, zero_fill, operands):
    if active is None:
        return compute(operands)
    return lax.cond(active, compute, zero_fill, operands)


def half(array, index_id, axis):
    size = array.shape[axis] // 2
    return lax.dynamic_slice_in_dim(array, index_id * size, size, axis)


def eliminate_whole(operands, place):
    row_id, col_id, diag_id = place
    pivot, below, above = operands
    inverse = inverse_of(pivot)
    below_col = half(below, col_id, 1)
    above_row = half(above, row_id, 0)
    solved = hdot(inverse, below_col)
    gram_down = hdot(half(below, row_id, 1), solved, ((0,), (0,)))
    gram_up = hdot(above_row, hdot(inverse, half(above, col_id, 0), ((1,), (1,))))
    return (log_of(inverse, place), gram_down, gram_up, -hdot(above_row, solved))


def eliminate(pivot_tile, below_tile, above_tile, active, place):
    half_width = pivot_tile.shape[0]
    log_zero = jnp.zeros((half_width // 2,), jnp.float32)
    tile_zero = jnp.zeros((half_width, half_width), jnp.float32)
    whole = whole_blocks(jnp.stack([pivot_tile, below_tile, above_tile]))
    return guarded(
        active,
        lambda operands: eliminate_whole(operands, place),
        lambda operands: (log_zero, tile_zero, tile_zero, tile_zero),
        (whole[0], whole[1], whole[2]),
    )


def final_log(pivot, place):
    return log_of(inverse_of(pivot), place)


def shards(precision_diag, precision_link):
    row_id = lax.axis_index("row")
    col_id = lax.axis_index("col")
    time_id = lax.axis_index("tm")
    place = (row_id, col_id, row_id * 2 + col_id)
    device_count = lax.axis_size("tm")
    pivot_low = precision_diag[0]
    pivot_high = precision_diag[1]
    link_low = precision_link[0]
    link_high = jnp.where(
        time_id == device_count - 1, jnp.zeros_like(precision_link[1]), precision_link[1]
    )
    log_high, gram_down, gram_up, link_low = eliminate(pivot_high, link_low, link_high, None, place)
    ahead_gram, from_below = send_later(gram_up, link_low, 1)
    pivot_low = pivot_low - gram_down - ahead_gram
    log_low = jnp.zeros_like(log_high)
    for level_num in range(1, LEVELS):
        stride = 2 ** (level_num - 1)
        position = time_id % (2 * stride)
        active = position == stride
        keeper = position == 0
        below_link = from_below
        log_now, gram_down, gram_up, link_new = eliminate(
            pivot_low, below_link, link_low, active, place
        )
        back_gram, back_link = shifted((gram_down, link_new), "tm", -stride)
        ahead_gram, from_below = send_later(gram_up, link_new, stride)
        log_low = jnp.where(active, log_now, log_low)
        pivot_low = pivot_low - back_gram - ahead_gram
        link_low = jnp.where(keeper, back_link, link_low)
    remaining = time_id % 2 ** (LEVELS - 1) == 0
    whole_pivot = whole_blocks(pivot_low[None])[0]
    log_final = lax.cond(
        remaining,
        lambda pivot: final_log(pivot, place),
        lambda pivot: jnp.zeros_like(log_low),
        whole_pivot,
    )
    log_low = jnp.where(remaining, log_final, log_low)
    pivots = jnp.stack([pivot_low, pivot_high])
    couplings = jnp.stack([link_low, link_high])
    logs = jnp.stack([log_low, log_high])
    return (pivots, couplings, logs)


def solution(mesh):
    in_specs = (P("tm", "row", "col"), P("tm", "row", "col"))
    out_specs = (P("tm", "row", "col"), P("tm", "row", "col"), P("tm", ("row", "col")))
    return jax.shard_map(shards, mesh=mesh, in_specs=in_specs, out_specs=out_specs, check_vma=False)
```

time: 1150 us -> 499 us (0.43)
  waiting for transfers between devices: 672 us -> 205 us
  other arithmetic: 242 us -> 11.6 us
  starting transfers between devices: 47.2 us -> 171 us
  blocking collectives: 83.7 us -> 8.41 us
  Pallas kernels: 0 us -> 48.7 us
  matrix products: 23.3 us -> 5.56 us
  local copies, waits for them, and re-layouts: 37.3 us -> 24 us
  loops' own time: 13.3 us -> 1.05 us
    all_gather x8 -> x4, waiting for transfers between devices: 623 us -> 116 us  [whole_blocks(): widened = lax.all_gather(stacked, 'col', axis=2, tiled=True)]
    another operation x36 -> x6, other arithmetic: 238 us -> 4.99 us  [eliminate(): whole = whole_blocks(jnp.stack([pivot_tile, below_tile, above_tile]))]
    ppermute x13, starting transfers between devices: 46.7 us -> 171 us  [shifted(): return lax.ppermute(array, axis, pairs)]
    all_gather x5, waiting for transfers between devices: 0.03 us -> 54.2 us  [whole_blocks(): return lax.all_gather(widened, 'row', axis=1, tiled=True)]
    pallas_call x0 -> x2, Pallas kernels: none -> 48.7 us  [inverse_of(): pl.pallas_call(inverse_kernel, out_shape=jax.ShapeDtypeStruct(pivot.shape...]
    all_gather x8 -> x0, blocking collectives: 39.4 us -> none  [the longest x4 30.4 us: eliminate(): above_rows = lax.all_gather(above_tile, 'col', axis=1, tiled=True)]
    all_gather x5 -> x1, blocking collectives: 44.3 us -> 8.41 us  [whole_blocks(): widened = lax.all_gather(stacked, 'col', axis=2, tiled=True)]
    another operation x52 -> x13, local copies, waits for them, and re-layouts: 25 us -> 6.57 us
  transfers between devices with their start and end apart: 26 -> 22, of which waited for: 16 -> 18; matrix products, arithmetic and copies ran while one was open for 1% -> 2% of each run, Pallas kernels for 0% -> 0%
where the time goes in v1:
time: 499 us; the launch traced here: 491 us
  waiting for transfers between devices  205 us (41%)
  starting transfers between devices  171 us (34%)
  Pallas kernels  48.7 us (10%)
  local copies, waits for them, and re-layouts  24 us (5%)
  between operations  14.7 us (3%)
  other arithmetic  11.6 us (2%)
  blocking collectives  8.41 us (2%)
  matrix products  5.56 us (1%)
    ppermute x13, starting transfers between devices, shifted(): return lax.ppermute(array, axis, pairs)  171 us
    all_gather x4, waiting for transfers between devices, whole_blocks(): widened = lax.all_gather(stacked, 'col', axis=2, tiled=True)  116 us
    all_gather x5, waiting for transfers between devices, whole_blocks(): return lax.all_gather(widened, 'row', axis=1, tiled=True)  54.2 us
    pallas_call x2, Pallas kernels, inverse_of(): pl.pallas_call(inverse_kernel, out_shape=jax.ShapeDtypeStruct(pivot.shape...  48.7 us
    ppermute x13, waiting for transfers between devices, shifted(): return lax.ppermute(array, axis, pairs)  34.8 us
    gather x2, local copies, waits for them, and re-layouts, log_of(): jnp.diagonal(inverse)  13 us
  transfers between devices with their start and end apart: 22, of which 18 were waited for; matrix products, arithmetic and copies ran while one was open for 2% of the time, Pallas kernels for 0%

profile of v1, /device:TPU:0, one launch (start us, length us, event | category | flops | bytes accessed | tf_op | source)
XLA Modules:
  0.0 490.6 jit_solution(13500497372836620092)
XLA Ops:
  10.4 30.0 %all-gather.12.cloned.1.call-done = f32[3,256,512]{2,1,0:T(8,128)} async-done(((f32[3,256,256]{2,1,0:T(8,128)}), f32[3,256,512]{2,1,0:T(8,128)}) %all-gather.12.cloned.1.call-update) | async-done | bytes 1572880 | tf_op jit(solution)/shard_map/all_gather | solution.py:98
  40.5 13.6 %all-gather.14.cloned.1.call-done = f32[3,512,512]{2,1,0:T(8,128)} async-done(((f32[3,256,512]{2,1,0:T(8,128)}), f32[3,512,512]{2,1,0:T(8,128)}) %all-gather.14.cloned.1.call-update) | async-done | bytes 3145744 | tf_op jit(solution)/shard_map/all_gather | solution.py:99
  57.4 24.3 %shard_map.49 = f32[512,512]{1,0:T(8,128)} custom-call(f32[512,512]{1,0:T(8,128)} %get-tuple-element.107.pivot_ref), custom_call_target="tpu_custom_call" | custom-call | tf_op jit(solution)/shard_map/pallas_call | solution.py:84
  96.1 3.9 collective-permute-done.1
  101.1 29.2 %all-gather.16.cloned.1.call-done = f32[3,256,512]{2,1,0:T(8,128)} async-done(((f32[3,256,256]{2,1,0:T(8,128)}), f32[3,256,512]{2,1,0:T(8,128)}) %all-gather.16.cloned.1.call-update) | async-done | bytes 1572880 | tf_op jit(solution)/shard_map/all_gather | solution.py:98
  130.4 13.5 %all-gather.18.cloned.1.call-done = f32[3,512,512]{2,1,0:T(8,128)} async-done(((f32[3,256,512]{2,1,0:T(8,128)}), f32[3,512,512]{2,1,0:T(8,128)}) %all-gather.18.cloned.1.call-update) | async-done | bytes 3145744 | tf_op jit(solution)/shard_map/all_gather | solution.py:99
  149.1 49.2 %collective-permute-start.3 = (f32[256,256]{1,0:T(8,128)}, f32[256,256]{1,0:T(8,128)S(1)}, u32[]{:S(2)}, u32[]{:S(2)}) collective-permute-start(f32[256,256]{1,0:T(8,128)} %get-tuple-element.86), channel_id=1, source_target_pairs={{0,4},{4,8},{8,12},{12,16},{16,20},{20,24},{24,28},{1,5},{5,9},{9,... | collective-permute-start | bytes 786440 | tf_op jit(solution)/shard_map/ppermute | solution.py:14
  198.2 4.8 collective-permute-start.4
  203.1 3.8 collective-permute-done.2
  206.9 5.9 %collective-permute-done.3 = f32[256,256]{1,0:T(8,128)S(1)} collective-permute-done((f32[256,256]{1,0:T(8,128)}, f32[256,256]{1,0:T(8,128)S(1)}, u32[]{:S(2)}, u32[]{:S(2)}) %collective-permute-start.3) | collective-permute-done | bytes 262176 | tf_op jit(solution)/shard_map/ppermute | solution.py:14
  214.0 4.5 collective-permute-done.4
  219.5 28.2 %all-gather.20.cloned.1.call-done = f32[3,256,512]{2,1,0:T(8,128)} async-done(((f32[3,256,256]{2,1,0:T(8,128)}), f32[3,256,512]{2,1,0:T(8,128)}) %all-gather.20.cloned.1.call-update) | async-done | bytes 1572880 | tf_op jit(solution)/shard_map/all_gather | solution.py:98
  247.7 13.5 %all-gather.22.cloned.1.call-done = f32[3,512,512]{2,1,0:T(8,128)} async-done(((f32[3,256,512]{2,1,0:T(8,128)}), f32[3,512,512]{2,1,0:T(8,128)}) %all-gather.22.cloned.1.call-update) | async-done | bytes 3145744 | tf_op jit(solution)/shard_map/all_gather | solution.py:99
  266.1 49.2 %collective-permute-start.7 = (f32[256,256]{1,0:T(8,128)}, f32[256,256]{1,0:T(8,128)S(1)}, u32[]{:S(2)}, u32[]{:S(2)}) collective-permute-start(f32[256,256]{1,0:T(8,128)} %get-tuple-element.89), channel_id=1, source_target_pairs={{0,8},{4,12},{8,16},{12,20},{16,24},{20,28},{1,9},{5,13},{9,17},{1... | collective-permute-start | bytes 786440 | tf_op jit(solution)/shard_map/ppermute | solution.py:14
  315.3 3.9 collective-permute-start.8
  328.3 28.7 %all-gather.24.cloned.1.call-done = f32[3,256,512]{2,1,0:T(8,128)} async-done(((f32[3,256,256]{2,1,0:T(8,128)}), f32[3,256,512]{2,1,0:T(8,128)}) %all-gather.24.cloned.1.call-update) | async-done | bytes 1572880 | tf_op jit(solution)/shard_map/all_gather | solution.py:98
  357.1 13.6 %all-gather.26.cloned.1.call-done = f32[3,512,512]{2,1,0:T(8,128)} async-done(((f32[3,256,512]{2,1,0:T(8,128)}), f32[3,512,512]{2,1,0:T(8,128)}) %all-gather.26.cloned.1.call-update) | async-done | bytes 3145744 | tf_op jit(solution)/shard_map/all_gather | solution.py:99
  374.5 49.0 %collective-permute-start.11 = (f32[256,256]{1,0:T(8,128)}, f32[256,256]{1,0:T(8,128)S(1)}, u32[]{:S(2)}, u32[]{:S(2)}) collective-permute-start(f32[256,256]{1,0:T(8,128)} %get-tuple-element.92), channel_id=1, source_target_pairs={{0,16},{4,20},{8,24},{12,28},{1,17},{5,21},{9,25},{13,29},{2,18},{... | collective-permute-start | bytes 786440 | tf_op jit(solution)/shard_map/ppermute | solution.py:14
  423.5 4.9 collective-permute-done.10
  430.8 8.4 %all-gather = f32[256,512]{1,0:T(8,128)} all-gather(f32[256,256]{1,0:T(8,128)S(1)} %subtract_subtract_fusion), channel_id=2, replica_groups=mesh['tm'=8,'row'=2,'col'=2] {'col'}, dimensions={1}, use_global_device_ids=true | all-gather | bytes 786432 | tf_op jit(solution)/shard_map/all_gather | solution.py:98
  440.5 4.5 gather_fusion.4
  449.9 33.2 %conditional.7 = (f32[128]{0:T(128)S(1)}) conditional(s32[]{:T(128)} %convert_element_type.15, () %tuple.44, (f32[1,512,512]{2,1,0:T(8,128)}, s32[]{:T(128)}) %tuple.82), branch_computations={%region_6.7_spmd, %region_7.8_spmd} | conditional | flops 2052 | bytes 15418 | solution.py:178
  450.1 24.3 %branch_1_fun.7 = f32[512,512]{1,0:T(8,128)} custom-call(f32[512,512]{1,0:T(8,128)} %bitcast.122), custom_call_target="tpu_custom_call" | custom-call | tf_op jit(solution)/shard_map/cond/branch_1_fun/pallas_call | solution.py:84
  474.5 8.5 %gather_fusion = f32[512]{0:T(512)S(1)} fusion(f32[512,512]{1,0:T(8,128)} %branch_1_fun.7, s32[512]{0:T(512)S(1)} %bitcast.112), kind=kCustom, calls=%fused_computation.3 | custom fusion | bytes 8192 | tf_op jit(solution)/shard_map/cond/branch_1_fun/jit(diagonal)/cond/branch_0_fun/gather | solution.py:94
  (100 shorter events, 62.7 us)
Async XLA Ops:
  7.2 33.3 %all-gather.12.cloned.1.call-start = ((), (), s32[]{:S(2)}) async-start(), calls=%async_computation | async-start | bytes 2359296 | tf_op jit(solution)/shard_map/all_gather | solution.py:98
  10.4 43.8 %all-gather.14.cloned.1.call-start = ((), (), s32[]{:S(2)}) async-start(), calls=%async_computation.1 | async-start | bytes 4718592 | tf_op jit(solution)/shard_map/all_gather | solution.py:99
  40.5 89.8 %all-gather.16.cloned.1.call-start = ((), (), s32[]{:S(2)}) async-start(), calls=%async_computation.2 | async-start | bytes 2359296 | tf_op jit(solution)/shard_map/all_gather | solution.py:98
  84.7 10.3 %collective-permute-start = (f32[256,256]{1,0:T(8,128)S(1)}, f32[256,256]{1,0:T(8,128)S(1)}, u32[]{:S(2)}, u32[]{:S(2)}) collective-permute-start(f32[256,256]{1,0:T(8,128)S(1)} %fusion.61), channel_id=1, source_target_pairs={{0,4},{4,8},{8,12},{12,16},{16,20},{20,24},{24,28},{1,5},{5,9},{9,... | collective-permute-start | bytes 786440 | tf_op jit(solution)/shard_map/ppermute | solution.py:14
  90.0 10.0 %collective-permute-start.1 = (f32[256,256]{1,0:T(8,128)S(1)}, f32[256,256]{1,0:T(8,128)S(1)}, u32[]{:S(2)}, u32[]{:S(2)}) collective-permute-start(f32[256,256]{1,0:T(8,128)S(1)} %convolution_negate_fusion.3), channel_id=1, source_target_pairs={{0,4},{4,8},{8,12},{12,16},{16,20},{20,24},{24,28},{1,5},{5,9},{9,... | collective-permute-start | bytes 786440 | tf_op jit(solution)/shard_map/ppermute | solution.py:14
  101.0 42.8 %all-gather.18.cloned.1.call-start = ((), (), s32[]{:S(2)}) async-start(), calls=%async_computation.3 | async-start | bytes 4718592 | tf_op jit(solution)/shard_map/all_gather | solution.py:99
  130.3 117.4 %all-gather.20.cloned.1.call-start = ((), (), s32[]{:S(2)}) async-start(), calls=%async_computation.4 | async-start | bytes 2359296 | tf_op jit(solution)/shard_map/all_gather | solution.py:98
  146.4 56.6 %collective-permute-start.5 = (f32[256,256]{1,0:T(8,128)}, f32[256,256]{1,0:T(8,128)S(1)}, u32[]{:S(2)}, u32[]{:S(2)}) collective-permute-start(f32[256,256]{1,0:T(8,128)} %get-tuple-element.87), channel_id=1, source_target_pairs={{4,0},{8,4},{12,8},{16,12},{20,16},{24,20},{28,24},{5,1},{9,5},{13... | collective-permute-start | bytes 786440 | tf_op jit(solution)/shard_map/ppermute | solution.py:14
  147.8 59.2 %collective-permute-start.2 = (f32[256,256]{1,0:T(8,128)}, f32[256,256]{1,0:T(8,128)S(1)}, u32[]{:S(2)}, u32[]{:S(2)}) collective-permute-start(f32[256,256]{1,0:T(8,128)} %get-tuple-element.85), channel_id=1, source_target_pairs={{4,0},{8,4},{12,8},{16,12},{20,16},{24,20},{28,24},{5,1},{9,5},{13... | collective-permute-start | bytes 786440 | tf_op jit(solution)/shard_map/ppermute | solution.py:14
  149.1 63.8 %collective-permute-start.3 = (f32[256,256]{1,0:T(8,128)}, f32[256,256]{1,0:T(8,128)S(1)}, u32[]{:S(2)}, u32[]{:S(2)}) collective-permute-start(f32[256,256]{1,0:T(8,128)} %get-tuple-element.86), channel_id=1, source_target_pairs={{0,4},{4,8},{8,12},{12,16},{16,20},{20,24},{24,28},{1,5},{5,9},{9,... | collective-permute-start | bytes 786440 | tf_op jit(solution)/shard_map/ppermute | solution.py:14
  198.2 20.2 %collective-permute-start.4 = (f32[256,256]{1,0:T(8,128)}, f32[256,256]{1,0:T(8,128)S(1)}, u32[]{:S(2)}, u32[]{:S(2)}) collective-permute-start(f32[256,256]{1,0:T(8,128)} %get-tuple-element.87), channel_id=1, source_target_pairs={{0,4},{4,8},{8,12},{12,16},{16,20},{20,24},{24,28},{1,5},{5,9},{9,... | collective-permute-start | bytes 786440 | tf_op jit(solution)/shard_map/ppermute | solution.py:14
  219.4 41.8 %all-gather.22.cloned.1.call-start = ((), (), s32[]{:S(2)}) async-start(), calls=%async_computation.5 | async-start | bytes 4718592 | tf_op jit(solution)/shard_map/all_gather | solution.py:99
  247.7 109.3 %all-gather.24.cloned.1.call-start = ((), (), s32[]{:S(2)}) async-start(), calls=%async_computation.6 | async-start | bytes 2359296 | tf_op jit(solution)/shard_map/all_gather | solution.py:98
  263.5 55.7 %collective-permute-start.9 = (f32[256,256]{1,0:T(8,128)}, f32[256,256]{1,0:T(8,128)S(1)}, u32[]{:S(2)}, u32[]{:S(2)}) collective-permute-start(f32[256,256]{1,0:T(8,128)} %get-tuple-element.90), channel_id=1, source_target_pairs={{8,0},{12,4},{16,8},{20,12},{24,16},{28,20},{9,1},{13,5},{17,9},{2... | collective-permute-start | bytes 786440 | tf_op jit(solution)/shard_map/ppermute | solution.py:14
  264.8 59.2 %collective-permute-start.6 = (f32[256,256]{1,0:T(8,128)}, f32[256,256]{1,0:T(8,128)S(1)}, u32[]{:S(2)}, u32[]{:S(2)}) collective-permute-start(f32[256,256]{1,0:T(8,128)} %get-tuple-element.88), channel_id=1, source_target_pairs={{8,0},{12,4},{16,8},{20,12},{24,16},{28,20},{9,1},{13,5},{17,9},{2... | collective-permute-start | bytes 786440 | tf_op jit(solution)/shard_map/ppermute | solution.py:14
  266.1 57.9 %collective-permute-start.7 = (f32[256,256]{1,0:T(8,128)}, f32[256,256]{1,0:T(8,128)S(1)}, u32[]{:S(2)}, u32[]{:S(2)}) collective-permute-start(f32[256,256]{1,0:T(8,128)} %get-tuple-element.89), channel_id=1, source_target_pairs={{0,8},{4,12},{8,16},{12,20},{16,24},{20,28},{1,9},{5,13},{9,17},{1... | collective-permute-start | bytes 786440 | tf_op jit(solution)/shard_map/ppermute | solution.py:14
  315.3 11.9 %collective-permute-start.8 = (f32[256,256]{1,0:T(8,128)}, f32[256,256]{1,0:T(8,128)S(1)}, u32[]{:S(2)}, u32[]{:S(2)}) collective-permute-start(f32[256,256]{1,0:T(8,128)} %get-tuple-element.90), channel_id=1, source_target_pairs={{0,8},{4,12},{8,16},{12,20},{16,24},{20,28},{1,9},{5,13},{9,17},{1... | collective-permute-start | bytes 786440 | tf_op jit(solution)/shard_map/ppermute | solution.py:14
  328.2 42.4 %all-gather.26.cloned.1.call-start = ((), (), s32[]{:S(2)}) async-start(), calls=%async_computation.7 | async-start | bytes 4718592 | tf_op jit(solution)/shard_map/all_gather | solution.py:99
  357.0 92.9 %all-gather.28.cloned.1.call-start = ((), (), s32[]{:S(2)}) async-start(), calls=%async_computation.8 | async-start | bytes 1572864 | tf_op jit(solution)/shard_map/all_gather | solution.py:99
  373.0 72.1 %copy-start.6 = (f32[1,256,256]{2,1,0:T(8,128)S(1)}, f32[1,256,256]{2,1,0:T(8,128)}, u32[]{:S(2)}) copy-start(f32[1,256,256]{2,1,0:T(8,128)} %copy-done.5) | copy-start | bytes 786436
  373.0 55.3 %collective-permute-start.10 = (f32[256,256]{1,0:T(8,128)}, f32[256,256]{1,0:T(8,128)S(1)}, u32[]{:S(2)}, u32[]{:S(2)}) collective-permute-start(f32[256,256]{1,0:T(8,128)} %get-tuple-element.91), channel_id=1, source_target_pairs={{16,0},{20,4},{24,8},{28,12},{17,1},{21,5},{25,9},{29,13},{18,2},{... | collective-permute-start | bytes 786440 | tf_op jit(solution)/shard_map/ppermute | solution.py:14
  374.5 74.6 %copy-start.8 = (f32[1,256,256]{2,1,0:T(8,128)S(1)}, f32[1,256,256]{2,1,0:T(8,128)}, u32[]{:S(2)}) copy-start(f32[1,256,256]{2,1,0:T(8,128)} %copy-done.7) | copy-start | bytes 786436
  374.5 55.3 %collective-permute-start.11 = (f32[256,256]{1,0:T(8,128)}, f32[256,256]{1,0:T(8,128)S(1)}, u32[]{:S(2)}, u32[]{:S(2)}) collective-permute-start(f32[256,256]{1,0:T(8,128)} %get-tuple-element.92), channel_id=1, source_target_pairs={{0,16},{4,20},{8,24},{12,28},{1,17},{5,21},{9,25},{13,29},{2,18},{... | collective-permute-start | bytes 786440 | tf_op jit(solution)/shard_map/ppermute | solution.py:14
  439.2 9.8 %collective-permute-start.12 = (f32[256,256]{1,0:T(8,128)}, f32[256,256]{1,0:T(8,128)S(1)}, u32[]{:S(2)}, u32[]{:S(2)}) collective-permute-start(f32[256,256]{1,0:T(8,128)} %get-tuple-element.93), channel_id=1, source_target_pairs={{16,0},{20,4},{24,8},{28,12},{17,1},{21,5},{25,9},{29,13},{18,2},{... | collective-permute-start | bytes 786440 | tf_op jit(solution)/shard_map/ppermute | solution.py:14
  (9 other events, 283.9 us)
Sparse Core Ops, SparseCore 0:
  10.5 29.8 all-gather.11
  42.0 12.1 all-gather.13
  101.1 29.0 all-gather.15
  131.7 12.1 all-gather.17
  219.5 28.0 all-gather.19
  249.1 12.1 all-gather.21
  328.4 28.5 all-gather.23
  358.5 12.1 all-gather.25
  439.3 8.9 all-gather.27

commit v2 on v1

v2 whole, which is shorter than its diff:
```python
import jax
import jax.numpy as jnp
from jax import lax
from jax.experimental import pallas as pl
from jax.experimental.pallas import tpu as pltpu
from jax.sharding import PartitionSpec as P

LEVELS = 4

LANES = 128
ROWS = 8


def hdot(left, right, dims=((1,), (0,))):
    return lax.dot_general(
        left, right, (dims, ((), ())), precision=lax.Precision.HIGHEST, preferred_element_type=jnp.float32
    )


def invert_lanes(block):
    sub = lax.broadcasted_iota(jnp.int32, (ROWS, LANES), 0)
    lane = lax.broadcasted_iota(jnp.int32, (ROWS, LANES), 1)
    strips = [block[ROWS * q : ROWS * (q + 1), :] for q in range(LANES // ROWS)]
    for p in range(len(strips)):
        base = ROWS * p
        spread = lambda strip: [
            jnp.broadcast_to(strip[:, base + j : base + j + 1], (ROWS, LANES)) for j in range(ROWS)
        ]
        inside = (lane >= base) & (lane < base + ROWS)
        panel = strips[p]
        cols = spread(panel)
        panel = jnp.where(inside, jnp.where(lane - base == sub, 1.0, 0.0), panel)
        for i in range(ROWS):
            here = sub == i
            scale = 1.0 / jnp.broadcast_to(cols[i][i : i + 1, :], (ROWS, LANES))
            factor = jnp.where(here, scale, -cols[i] * scale)
            panel = jnp.where(here, 0.0, panel) + factor * panel[i : i + 1, :]
            for j in range(i + 1, ROWS):
                cols[j] = jnp.where(here, 0.0, cols[j]) + factor * cols[j][i : i + 1, :]
        order = [q for q in range(p + 1, len(strips))] + [q for q in range(p)]
        for q in order:
            terms = [c * panel[j : j + 1, :] for j, c in enumerate(spread(strips[q]))]
            while len(terms) > 1:
                terms = [terms[m] + terms[m + 1] for m in range(0, len(terms), 2)]
            strips[q] = jnp.where(inside, 0.0, strips[q]) - terms[0]
        strips[p] = panel
    return jnp.concatenate(strips, axis=0)


def invert_ref(work, between):
    node_count = work.shape[0]

    def step(k, carry):
        between(k)
        here = pl.ds(pl.multiple_of(k * LANES, LANES), LANES)
        inverse = invert_lanes(work[here, here])
        solved = hdot(inverse, work[here, :])
        column = work[:, here]
        work[:, here] = jnp.zeros((node_count, LANES), jnp.float32)
        row_block = lax.broadcasted_iota(jnp.int32, (node_count, LANES), 0) // LANES
        column = jnp.where(row_block == k, 0.0, column)
        col_block = lax.broadcasted_iota(jnp.int32, (LANES, node_count), 1) // LANES
        wide = jnp.concatenate([inverse] * (node_count // LANES), axis=1)
        solved = jnp.where(col_block == k, wide, solved)
        work[...] = work[...] - hdot(column, solved)
        work[here, :] = solved
        return carry

    lax.fori_loop(0, node_count // LANES, step, 0)


def cyclic_kernel(
    diag_ref, link_ref, pivot_ref, coupling_ref, log_ref,
    whole, work, made, ahead, back,
    x_send, x_recv, r_send, r_recv, f_send, f_recv,
    up_send, down_send, ahead_recv, back_recv,
):
    time_id, row_id, col_id = lax.axis_index("tm"), lax.axis_index("row"), lax.axis_index("col")
    times = lax.axis_size("tm")
    half = diag_ref.shape[1]
    node_count = 2 * half
    blocks = node_count // LANES
    reach = LEVELS - 1
    depth = sum((lax.rem(time_id, 2**j) == 0).astype(jnp.int32) for j in range(1, reach + 1))
    stride = sum(jnp.where(depth == j, 2**j, 0) for j in range(reach))
    mesh_id = pl.DeviceIdType.MESH

    def part(index):
        return pl.ds(pl.multiple_of(index * half, LANES), half)

    mine_rows, mine_cols = part(row_id), part(col_id)
    other_rows, other_cols = part(1 - row_id), part(1 - col_id)

    barrier = pltpu.get_barrier_semaphore()
    pl.semaphore_signal(barrier, inc=1, device_id={"col": 1 - col_id}, device_id_type=mesh_id)
    pl.semaphore_signal(barrier, inc=1, device_id={"row": 1 - row_id}, device_id_type=mesh_id)
    greeted = 2
    for j in range(reach):
        for by in (-(2**j), 2**j):
            near = (depth >= j) & (time_id + by >= 0) & (time_id + by < times)

            @pl.when(near)
            def _(by=by):
                pl.semaphore_signal(barrier, inc=1, device_id={"tm": time_id + by}, device_id_type=mesh_id)

            greeted = greeted + near.astype(jnp.int32)
    pl.semaphore_wait(barrier, greeted)

    def copy(src, dst, send, recv, target):
        return pltpu.make_async_remote_copy(
            src_ref=src, dst_ref=dst, send_sem=send, recv_sem=recv, device_id=target, device_id_type=mesh_id
        )

    def phase(ph, carry):
        first = ph == 0
        later = ph == 1
        solving = first | (depth < reach)
        on_diag = row_id == col_id

        def x_copy(a):
            tile = whole.at[ph, a, mine_rows, mine_cols]
            return copy(tile, tile, x_send.at[ph, a], x_recv.at[ph, a], {"col": 1 - col_id})

        def r_copy(a):
            tile = whole.at[ph, a, mine_rows, mine_cols]
            return copy(tile, tile, r_send.at[ph, a], r_recv.at[ph, a], {"row": 1 - row_id})

        def f_copy(a):
            tile = whole.at[ph, a, mine_rows, other_cols]
            return copy(tile, tile, f_send.at[ph, a], f_recv.at[ph, a], {"row": 1 - row_id})

        def up_copy(kind, source, level, by):
            return copy(
                made.at[ph, source], ahead.at[level, kind], up_send.at[ph, kind], ahead_recv.at[level, kind],
                {"tm": time_id + by},
            )

        def down_copy(kind, source, level, by):
            return copy(
                made.at[ph, source], back.at[level, kind], down_send.at[kind], back_recv.at[level, kind],
                {"tm": time_id - by},
            )

        def received(kind, level):
            by = 1 if level == 0 else 2 ** (level - 1)

            def from_below(use):
                @pl.when((depth >= level) & (time_id >= by))
                def _():
                    up_copy(kind, 0, level, 0).wait_recv()
                    use(ahead)

            def from_above(use):
                if level > 0:

                    @pl.when(depth >= level)
                    def _():
                        down_copy(kind, 0, level, 0).wait_recv()
                        use(back)

            return from_below, from_above

        @pl.when(first)
        def _():
            whole[0, 0, mine_rows, mine_cols] = diag_ref[1]
            pivot_ref[1] = diag_ref[1]
            high = jnp.where(time_id == times - 1, 0.0, link_ref[1])
            coupling_ref[1] = high
            whole[0, 1, mine_rows, mine_cols] = link_ref[0]
            whole[0, 2, mine_rows, mine_cols] = high

        @pl.when(later)
        def _():
            pivot_ref[0] = diag_ref[0] - made[0, 1]
            for level in range(LEVELS):
                def subtract(source, level=level):
                    pivot_ref[0] = pivot_ref[0] - source[level, 0]

                for arrival in received(0, level):
                    arrival(subtract)
            whole[1, 0, mine_rows, mine_cols] = pivot_ref[0]

        @pl.when(on_diag)
        def _():
            x_copy(0).start()

        r_copy(0).start()
        r_copy(0).wait_recv()

        @pl.when(jnp.logical_not(on_diag))
        def _():
            x_copy(0).wait_recv()
            f_copy(0).start()

        @pl.when(on_diag)
        def _():
            f_copy(0).wait_recv()

        work[:, mine_cols] = whole[ph, 0, :, mine_cols]
        far = part(1 - col_id)
        work[far, other_cols] = whole[ph, 0, far, other_cols]
        work[part(col_id), other_cols] = whole[ph, 0, far, mine_cols].T

        def between(k):
            @pl.when(k == 1)
            def _():
                @pl.when(later)
                def _():
                    coupling_ref[0] = made[0, 2]
                    for level in range(LEVELS):
                        def place_below(source, level=level):
                            whole[1, 1, mine_rows, mine_cols] = source[level, 1]

                        def place_above(source, level=level):
                            coupling_ref[0] = source[level, 1]

                        from_below, from_above = received(1, level)
                        from_below(place_below)
                        from_above(place_above)
                    whole[1, 2, mine_rows, mine_cols] = coupling_ref[0]

                @pl.when(solving)
                def _():
                    for a in (1, 2):
                        x_copy(a).start()
                        r_copy(a).start()

            @pl.when((k == blocks - 1) & solving)
            def _():
                for a in (1, 2):
                    x_copy(a).wait_recv()
                    f_copy(a).start()

        invert_ref(work, between)

        spot = pl.ds(pl.multiple_of((2 * row_id + col_id) * (node_count // 4), LANES), node_count // 4)
        corner = work[spot, spot]
        same = lax.broadcasted_iota(jnp.int32, corner.shape, 0) == lax.broadcasted_iota(jnp.int32, corner.shape, 1)
        log_ref[pl.ds(1 - ph, 1), :] = jnp.log(jnp.sum(jnp.where(same, corner, 0.0), axis=0, keepdims=True))

        @pl.when(solving)
        def _():
            for a in (1, 2):
                r_copy(a).wait_recv()
                f_copy(a).wait_recv()
            above_row = whole[ph, 2, mine_rows, :]
            level = jnp.where(first, 0, depth + 1)
            by = jnp.where(first, 1, stride)
            goes_up = time_id + by < times
            reached = hdot(work[...], whole[ph, 2, part(col_id), :], ((1,), (1,)))
            made[ph, 0] = hdot(above_row, reached)

            @pl.when(goes_up)
            def _():
                up_copy(0, 0, level, by).start()

            solved = hdot(work[...], whole[ph, 1, :, mine_cols])
            made[ph, 1] = hdot(whole[ph, 1, :, part(row_id)], solved, ((0,), (0,)))

            @pl.when(later)
            def _():
                down_copy(0, 1, level, by).start()

            made[ph, 2] = -hdot(above_row, solved)

            @pl.when(goes_up)
            def _():
                up_copy(1, 2, level, by).start()

            @pl.when(later)
            def _():
                down_copy(1, 2, level, by).start()

            for a in (1, 2):
                x_copy(a).wait_send()
                r_copy(a).wait_send()
                f_copy(a).wait_send()

        r_copy(0).wait_send()

        @pl.when(on_diag)
        def _():
            x_copy(0).wait_send()

        @pl.when(jnp.logical_not(on_diag))
        def _():
            f_copy(0).wait_send()

        @pl.when(later)
        def _():
            @pl.when(time_id + 1 < times)
            def _():
                for kind in (0, 1):
                    copy(
                        made.at[0, 2 * kind], ahead.at[0, kind], up_send.at[0, kind], ahead_recv.at[0, kind],
                        {"tm": time_id + 1},
                    ).wait_send()

            @pl.when(depth < reach)
            def _():
                for kind in (0, 1):
                    down_copy(kind, 1 + kind, depth + 1, stride).wait_send()

                    @pl.when(time_id + stride < times)
                    def _(kind=kind):
                        up_copy(kind, 2 * kind, depth + 1, stride).wait_send()

        return carry

    lax.fori_loop(0, 2, phase, 0)


def shards(precision_diag, precision_link):
    half = precision_diag.shape[1]
    node_count = 2 * half
    vmem = pl.BlockSpec(memory_space=pltpu.VMEM)
    dma = pltpu.SemaphoreType.DMA
    tile = (half, half)
    stack = jax.ShapeDtypeStruct(precision_diag.shape, jnp.float32)
    return pl.pallas_call(
        cyclic_kernel,
        out_shape=(stack, stack, jax.ShapeDtypeStruct((2, node_count // 4), jnp.float32)),
        in_specs=[vmem, vmem],
        out_specs=(vmem, vmem, vmem),
        scratch_shapes=[
            pltpu.VMEM((2, 3, node_count, node_count), jnp.float32),
            pltpu.VMEM((node_count, node_count), jnp.float32),
            pltpu.VMEM((2, 3) + tile, jnp.float32),
            pltpu.VMEM((LEVELS, 2) + tile, jnp.float32),
            pltpu.VMEM((LEVELS, 2) + tile, jnp.float32),
            dma((2, 3)), dma((2, 3)), dma((2, 3)), dma((2, 3)), dma((2, 3)), dma((2, 3)),
            dma((2, 2)), dma((2,)), dma((LEVELS, 2)), dma((LEVELS, 2)),
        ],
        compiler_params=pltpu.CompilerParams(collective_id=0, has_side_effects=True),
    )(precision_diag, precision_link)


def solution(mesh):
    in_specs = (P("tm", "row", "col"), P("tm", "row", "col"))
    out_specs = (P("tm", "row", "col"), P("tm", "row", "col"), P("tm", ("row", "col")))
    return jax.shard_map(shards, mesh=mesh, in_specs=in_specs, out_specs=out_specs, check_vma=False)
```

time: 499 us -> 218 us (0.44); the launches traced: 491 us -> 217 us
  waiting for transfers between devices: 205 us -> 0 us
  starting transfers between devices: 171 us -> 0 us
  Pallas kernels: 48.7 us -> 213 us
  local copies, waits for them, and re-layouts: 24 us -> 3.29 us
  between operations: 14.7 us -> 0.65 us
  other arithmetic: 11.6 us -> 0 us
  blocking collectives: 8.41 us -> 0 us
  matrix products: 5.56 us -> 0 us
    ppermute x13 -> x0, starting transfers between devices: 171 us -> none  [shifted(): return lax.ppermute(array, axis, pairs)]
    all_gather x9 -> x0, waiting for transfers between devices: 170 us -> none  [the longest x4 116 us: whole_blocks(): widened = lax.all_gather(stacked, 'col', axis=2, tiled=True)]
    pallas_call x2 -> x1, Pallas kernels: 48.7 us -> 213 us  [shards(): pl.pallas_call(cyclic_kernel, out_shape=(stack, stack, jax.ShapeDtypeStru...]
    ppermute x13 -> x0, waiting for transfers between devices: 34.8 us -> none  [shifted(): return lax.ppermute(array, axis, pairs)]
    gather x2 -> x0, local copies, waits for them, and re-layouts: 13 us -> none  [log_of(): jnp.diagonal(inverse)]
    all_gather x1 -> x0, blocking collectives: 8.41 us -> none  [whole_blocks(): widened = lax.all_gather(stacked, 'col', axis=2, tiled=True)]
    another operation x11 -> x0, other arithmetic: 7.26 us -> none  [the longest x6 4.99 us: eliminate(): whole = whole_blocks(jnp.stack([pivot_tile, below_tile, above_tile]))]
    another operation x13 -> x0, local copies, waits for them, and re-layouts: 6.57 us -> none
  transfers between devices with their start and end apart: 22 -> 0, of which waited for: 18 -> 0; matrix products, arithmetic and copies ran while one was open for 2% -> 0% of each run, Pallas kernels for 0% -> 0%
where the time goes in v2:
time: 218 us; the launch traced here: 217 us
  Pallas kernels  213 us (98%)
  local copies, waits for them, and re-layouts  3.29 us (2%)
    pallas_call x1, Pallas kernels, shards(): pl.pallas_call(cyclic_kernel, out_shape=(stack, stack, jax.ShapeDtypeStru...  213 us

profile of v2, /device:TPU:0, one launch (start us, length us, event | category | flops | bytes accessed | tf_op | source)
XLA Modules:
  0.0 217.4 jit_solution(6821846618457940434)
XLA Ops:
  0.6 213.4 %shard_map.49 = (f32[2,256,256]{2,1,0:T(8,128)}, f32[2,256,256]{2,1,0:T(8,128)}, f32[2,128]{1,0:T(2,128)}) custom-call(f32[2,256,256]{2,1,0:T(8,128)} %diag_ref.1, f32[2,256,256]{2,1,0:T(8,128)} %link_ref.1), custom_call_target="tpu_custom_call" | custom-call | tf_op jit(solution)/shard_map/pallas_call | solution.py:320
  214.1 0.0 copy-start
  214.1 1.9 copy.8
  216.0 0.0 copy-done
  216.0 0.0 copy-start.1
  216.0 0.8 copy.9
  216.8 0.0 copy-done.1
  216.8 0.6 copy.10
Async XLA Ops:
  214.1 1.9 copy-start
  216.0 0.8 copy-start.1

commit v3 on v2

--- a/solution.py
+++ b/solution.py
@@ -9,6 +9,7 @@
 
 LANES = 128
 ROWS = 8
+GROUP = 32
 
 
 def hdot(left, right, dims=((1,), (0,))):
@@ -17,52 +18,113 @@
     )
 
 
-def invert_lanes(block):
+def split_three(array):
+    high = array.astype(jnp.bfloat16)
+    rest = array - high.astype(jnp.float32)
+    middle = rest.astype(jnp.bfloat16)
+    return high, middle, (rest - middle.astype(jnp.float32)).astype(jnp.bfloat16)
+
+
+def packed_dot(left, right):
+    high, middle, low = split_three(left)
+    first, second, third = split_three(right)
+    wide = jnp.concatenate([high, high, middle, middle, high, low], axis=1)
+    tall = jnp.concatenate([first, second, first, second, third, first], axis=0)
+    return jnp.dot(wide, tall, preferred_element_type=jnp.float32)
+
+
+def sweep_group(strips, start):
     sub = lax.broadcasted_iota(jnp.int32, (ROWS, LANES), 0)
     lane = lax.broadcasted_iota(jnp.int32, (ROWS, LANES), 1)
-    strips = [block[ROWS * q : ROWS * (q + 1), :] for q in range(LANES // ROWS)]
-    for p in range(len(strips)):
-        base = ROWS * p
-        spread = lambda strip: [
-            jnp.broadcast_to(strip[:, base + j : base + j + 1], (ROWS, LANES)) for j in range(ROWS)
+    pick = lambda strip, row: jnp.broadcast_to(strip[row : row + 1, :], (ROWS, LANES))
+    strips = list(strips)
+    count = len(strips)
+
+    def spread(strip, p):
+        return [
+            jnp.broadcast_to(strip[:, start + ROWS * p + j : start + ROWS * p + j + 1], (ROWS, LANES)) for j in range(ROWS)
         ]
+
+    def total(terms):
+        while len(terms) > 1:
+            terms = [terms[m] + terms[m + 1] for m in range(0, len(terms), 2)]
+        return terms[0]
+
+    cols = spread(strips[0], 0)
+    for p in range(count):
+        base = start + ROWS * p
         inside = (lane >= base) & (lane < base + ROWS)
-        panel = strips[p]
-        cols = spread(panel)
-        panel = jnp.where(inside, jnp.where(lane - base == sub, 1.0, 0.0), panel)
-        for i in range(ROWS):
-            here = sub == i
-            scale = 1.0 / jnp.broadcast_to(cols[i][i : i + 1, :], (ROWS, LANES))
-            factor = jnp.where(here, scale, -cols[i] * scale)
-            panel = jnp.where(here, 0.0, panel) + factor * panel[i : i + 1, :]
-            for j in range(i + 1, ROWS):
-                cols[j] = jnp.where(here, 0.0, cols[j]) + factor * cols[j][i : i + 1, :]
-        order = [q for q in range(p + 1, len(strips))] + [q for q in range(p)]
-        for q in order:
-            terms = [c * panel[j : j + 1, :] for j, c in enumerate(spread(strips[q]))]
-            while len(terms) > 1:
-                terms = [terms[m] + terms[m + 1] for m in range(0, len(terms), 2)]
-            strips[q] = jnp.where(inside, 0.0, strips[q]) - terms[0]
+        panel = jnp.where(inside, jnp.where(lane - base == sub, 1.0, 0.0), strips[p])
+        if p + 1 < count:
+            ahead_cols = spread(strips[p], p + 1)
+            next_left = spread(strips[p + 1], p)
+            next_cols = spread(strips[p + 1], p + 1)
+        for i in range(0, ROWS, 2):
+            first, second = cols[i], cols[i + 1]
+            on_first, on_second = sub == i, sub == i + 1
+            outside = (sub < i) | (sub > i + 1)
+            a, b = pick(first, i), pick(first, i + 1)
+            d = pick(second, i + 1)
+            det = a * d - b * b
+            scale = pl.reciprocal(det, approx=True)
+            left = jnp.where(on_first, d, jnp.where(on_second, -b, second * b - first * d))
+            right = jnp.where(on_second, a, jnp.where(on_first, -b, first * b - second * a))
+            scale = scale * (2.0 - det * scale)
+            apply = lambda strip: jnp.where(outside, strip, 0.0) + scale * (left * pick(strip, i) + right * pick(strip, i + 1))
+            panel = apply(panel)
+            for j in range(i + 2, ROWS):
+                cols[j] = apply(cols[j])
+            if p + 1 < count:
+                ahead_cols = [apply(strip) for strip in ahead_cols]
+        if p + 1 < count:
+            cols = [
+                next_cols[j] - total([next_left[m] * pick(ahead_cols[j], m) for m in range(ROWS)])
+                for j in range(ROWS)
+            ]
+        for q in [q for q in range(p + 1, count)] + [q for q in range(p)]:
+            left_cols = next_left if q == p + 1 else spread(strips[q], p)
+            strips[q] = jnp.where(inside, 0.0, strips[q]) - total(
+                [c * pick(panel, j) for j, c in enumerate(left_cols)]
+            )
         strips[p] = panel
-    return jnp.concatenate(strips, axis=0)
-
-
-def invert_ref(work, between):
+    return strips
+
+
+def invert_lanes(block):
+    lane = lax.broadcasted_iota(jnp.int32, (LANES, LANES), 1)
+    for start in range(0, LANES, GROUP):
+        strips = [block[start + ROWS * q : start + ROWS * (q + 1), :] for q in range(GROUP // ROWS)]
+        solved = sweep_group(strips, start)
+        inside = (lane >= start) & (lane < start + GROUP)
+        above = [jnp.zeros((start, LANES), jnp.float32)] if start else []
+        rest = LANES - start - GROUP
+        below = [jnp.zeros((rest, LANES), jnp.float32)] if rest else []
+        padded = jnp.concatenate(above + solved + below, axis=0)
+        update = packed_dot(jnp.where(inside, block, 0.0), padded)
+        block = jnp.where(inside, 0.0, block) - update
+        block = jnp.concatenate(
+            ([block[:start, :]] if start else []) + solved + ([block[start + GROUP :, :]] if rest else []), axis=0
+        )
+    return block
+
+
+def invert_ref(work, between, first_block=0):
     node_count = work.shape[0]
 
     def step(k, carry):
         between(k)
-        here = pl.ds(pl.multiple_of(k * LANES, LANES), LANES)
+        block_id = lax.rem(k + first_block, node_count // LANES)
+        here = pl.ds(pl.multiple_of(block_id * LANES, LANES), LANES)
         inverse = invert_lanes(work[here, here])
-        solved = hdot(inverse, work[here, :])
+        solved = packed_dot(inverse, work[here, :])
         column = work[:, here]
         work[:, here] = jnp.zeros((node_count, LANES), jnp.float32)
         row_block = lax.broadcasted_iota(jnp.int32, (node_count, LANES), 0) // LANES
-        column = jnp.where(row_block == k, 0.0, column)
+        column = jnp.where(row_block == block_id, 0.0, column)
         col_block = lax.broadcasted_iota(jnp.int32, (LANES, node_count), 1) // LANES
         wide = jnp.concatenate([inverse] * (node_count // LANES), axis=1)
-        solved = jnp.where(col_block == k, wide, solved)
-        work[...] = work[...] - hdot(column, solved)
+        solved = jnp.where(col_block == block_id, wide, solved)
+        work[...] = work[...] - packed_dot(column, solved)
         work[here, :] = solved
         return carry
 
@@ -187,22 +249,26 @@
         r_copy(0).start()
         r_copy(0).wait_recv()
 
-        @pl.when(jnp.logical_not(on_diag))
-        def _():
-            x_copy(0).wait_recv()
-            f_copy(0).start()
-
-        @pl.when(on_diag)
-        def _():
-            f_copy(0).wait_recv()
-
         work[:, mine_cols] = whole[ph, 0, :, mine_cols]
         far = part(1 - col_id)
-        work[far, other_cols] = whole[ph, 0, far, other_cols]
+        work[far, other_cols] = jnp.zeros((half, half), jnp.float32)
         work[part(col_id), other_cols] = whole[ph, 0, far, mine_cols].T
 
         def between(k):
-            @pl.when(k == 1)
+            @pl.when((k == 1) & jnp.logical_not(on_diag))
+            def _():
+                x_copy(0).wait_recv()
+                f_copy(0).start()
+
+            @pl.when(k == blocks // 2)
+            def _():
+                @pl.when(on_diag)
+                def _():
+                    f_copy(0).wait_recv()
+
+                work[far, other_cols] = work[far, other_cols] + whole[ph, 0, far, other_cols]
+
+            @pl.when(k == jnp.where(first, 0, 1))
             def _():
                 @pl.when(later)
                 def _():
@@ -221,17 +287,16 @@
 
                 @pl.when(solving)
                 def _():
-                    for a in (1, 2):
+                    for a in (2, 1):
                         x_copy(a).start()
                         r_copy(a).start()
 
             @pl.when((k == blocks - 1) & solving)
             def _():
-                for a in (1, 2):
-                    x_copy(a).wait_recv()
-                    f_copy(a).start()
-
-        invert_ref(work, between)
+                x_copy(2).wait_recv()
+                f_copy(2).start()
+
+        invert_ref(work, between, col_id * (blocks // 2))
 
         spot = pl.ds(pl.multiple_of((2 * row_id + col_id) * (node_count // 4), LANES), node_count // 4)
         corner = work[spot, spot]
@@ -240,9 +305,10 @@
 
         @pl.when(solving)
         def _():
-            for a in (1, 2):
-                r_copy(a).wait_recv()
-                f_copy(a).wait_recv()
+            x_copy(1).wait_recv()
+            f_copy(1).start()
+            r_copy(2).wait_recv()
+            f_copy(2).wait_recv()
             above_row = whole[ph, 2, mine_rows, :]
             level = jnp.where(first, 0, depth + 1)
             by = jnp.where(first, 1, stride)
@@ -254,7 +320,9 @@
             def _():
                 up_copy(0, 0, level, by).start()
 
+            r_copy(1).wait_recv()
             solved = hdot(work[...], whole[ph, 1, :, mine_cols])
+            f_copy(1).wait_recv()
             made[ph, 1] = hdot(whole[ph, 1, :, part(row_id)], solved, ((0,), (0,)))
 
             @pl.when(later)

time: 218 us -> 167 us (0.77)
  Pallas kernels: 213 us -> 162 us
    pallas_call x1, Pallas kernels: 213 us -> 162 us  [shards(): pl.pallas_call(cyclic_kernel, out_shape=(stack, stack, jax.ShapeDtypeStru...]
where the time goes in v3:
time: 167 us; the launch traced here: 166 us
  Pallas kernels  162 us (97%)
  local copies, waits for them, and re-layouts  3.29 us (2%)
    pallas_call x1, Pallas kernels, shards(): pl.pallas_call(cyclic_kernel, out_shape=(stack, stack, jax.ShapeDtypeStru...  162 us

profile of v3, /device:TPU:0, one launch (start us, length us, event | category | flops | bytes accessed | tf_op | source)
XLA Modules:
  0.0 165.7 jit_solution(12614360791967803198)
XLA Ops:
  0.6 161.8 %shard_map.49 = (f32[2,256,256]{2,1,0:T(8,128)}, f32[2,256,256]{2,1,0:T(8,128)}, f32[2,128]{1,0:T(2,128)}) custom-call(f32[2,256,256]{2,1,0:T(8,128)} %diag_ref.1, f32[2,256,256]{2,1,0:T(8,128)} %link_ref.1), custom_call_target="tpu_custom_call" | custom-call | tf_op jit(solution)/shard_map/pallas_call | solution.py:388
  162.4 0.0 copy-start
  162.5 1.9 %copy.8 = f32[2,256,256]{2,1,0:T(8,128)} copy(f32[2,256,256]{2,1,0:T(8,128)} %get-tuple-element.6) | data formatting | bytes 1048576
  164.4 0.0 copy-done
  164.4 0.0 copy-start.1
  164.4 0.8 copy.9
  165.2 0.0 copy-done.1
  165.2 0.6 copy.10
Async XLA Ops:
  162.4 1.9 %copy-start = (f32[2,256,256]{2,1,0:T(8,128)S(1)}, f32[2,256,256]{2,1,0:T(8,128)}, u32[]{:S(2)}) copy-start(f32[2,256,256]{2,1,0:T(8,128)} %get-tuple-element.7) | copy-start | bytes 1572868
  164.4 0.8 copy-start.1
